TPU v7x, 32 devices: a whole 2x2x4 slice. The times are simulated.
32 devices in a mesh: section: 4 (over y, x), dp: 8 (over z, core).
Axes of the slice: x: 2, y: 2, z: 4, core: 2. Of those that a mesh axis runs over, the one named last changes fastest.
Arguments:
- inputs: bfloat16 [16, 128, 3072], P('dp'), may hold values from -6 to 6
- sample_ids: int32 [8, 2], P('dp'), may hold values from 0 to 1, each once within a row
- stored: bfloat16 [4, 2, 16, 128, 3072], P('section', None, 'dp'), may hold values from -4 to 4, as said below
- weight: bfloat16 [4, 3072, 3072], P('section'), may hold values from -0.109375 to 0.109375
- norm_gain: float32 [4, 3072], P('section'), may hold values from 0.1 to 1.9
Outputs:
- section_outputs: bfloat16 [4, 16, 128, 3072], P('section', 'dp')
- weight_grads: bfloat16 [4, 3072, 3072], P('section', 'dp')
Inputs may be any that keep to these rules, and one draw needn't show every extreme that they name: `sample_ids`: each row names each of the replica's 2 samples once. `stored`: copy 0 of section s equals copy 1 of section s - 1, and copy 0 of section 0 equals copy 1 of the last section.
All inputs are finite; a program needn't handle non-finite values.
Results may differ from a plain program's by a relative error of at most 0.024.
Values may be sent and summed in bfloat16 or wider, within the bound.
A program may use at most 192 MiB of HBM per device.

v0:
```python
from functools import partial
import math

import jax
import jax.numpy as jnp
from jax import lax
from jax.experimental import pallas as pl
from jax.experimental.pallas import tpu as pltpu
from jax.sharding import PartitionSpec as P

epsilon = 1e-05
delta_bound = 2.0


def from_behind(shard, axis, by):
    length = lax.axis_size(axis)
    pairs = [(i, i + by) for i in range(length) if 0 <= i + by < length]
    return lax.ppermute(shard, axis, pairs)


def activate(values):
    return jax.nn.gelu(values, approximate=False)


def normalize(state, norm_gain):
    average = jnp.mean(state, axis=-1, keepdims=True)
    centred = state - average
    variance = jnp.mean(centred * centred, axis=-1, keepdims=True)
    return centred * lax.rsqrt(variance + epsilon) * norm_gain


def forward_layer(state, layer_gain, layer_weight):
    normed = normalize(state, layer_gain).astype(jnp.bfloat16)
    preact = jnp.dot(normed, layer_weight, preferred_element_type=jnp.float32)
    return (normed, preact)


def pick(table, index):
    return lax.dynamic_index_in_dim(table, index, 0, keepdims=False)


def place(table, value, index):
    return lax.dynamic_update_index_in_dim(table, value, index, 0)


def per_device(inputs, sample_ids, stored, weight, norm_gain):
    num_sections = lax.axis_size("section")
    section_pos = lax.axis_index("section")
    num_batches, tokens, width = inputs.shape
    rows_total = num_batches * tokens
    layer_weight = weight[0]
    layer_gain = norm_gain[0]
    own_ids = sample_ids[0]
    recv_store = stored[0, 0]
    send_store = stored[0, 1]
    steps_total = num_batches + num_sections - 1
    is_first = section_pos == 0
    is_last = section_pos == num_sections - 1
    loss_scale = 1.0 / math.sqrt(lax.axis_size("dp") * rows_total)
    zero_act = jnp.zeros((tokens, width), jnp.bfloat16)
    stash_init = {
        "states": jnp.zeros((num_batches, tokens, width), jnp.float32),
        "results": jnp.zeros((num_batches, tokens, width), jnp.bfloat16),
    }
    stash_init["normed"] = jnp.zeros((num_batches, tokens, width), jnp.bfloat16)
    stash_init["preact"] = jnp.zeros((num_batches, tokens, width), jnp.float32)

    def forward_step(step, carry):
        incoming, stash = carry
        batch = step - section_pos
        valid = jnp.logical_and(batch >= 0, batch < num_batches)
        slot = jnp.clip(batch, 0, num_batches - 1)
        sample = pick(own_ids, slot)

        def forward_compute(stash_now):
            given = pick(inputs, slot).astype(jnp.float32)
            rebuilt = pick(recv_store, sample).astype(jnp.float32) + incoming.astype(jnp.float32)
            state = jnp.where(is_first, given, rebuilt)
            normed, preact = forward_layer(state, layer_gain, layer_weight)
            result = state + activate(preact)
            reference_copy = pick(send_store, sample).astype(jnp.float32)
            clipped = jnp.clip(result - reference_copy, -delta_bound, delta_bound).astype(
                jnp.bfloat16
            )
            updated = dict(stash_now)
            updated["states"] = place(stash_now["states"], state, slot)
            updated["results"] = place(stash_now["results"], result.astype(jnp.bfloat16), slot)
            updated["normed"] = place(stash_now["normed"], normed, slot)
            updated["preact"] = place(stash_now["preact"], preact, slot)
            return (clipped, updated)

        def forward_skip(stash_now):
            return (zero_act, stash_now)

        clipped, stash = lax.cond(valid, forward_compute, forward_skip, stash)
        outgoing = from_behind(clipped, "section", 1)
        return (outgoing, stash)

    last_incoming, stash = lax.fori_loop(0, steps_total, forward_step, (zero_act, stash_init))
    normed_init = stash["normed"]
    grad_init = jnp.zeros((num_batches, tokens, width), jnp.bfloat16)

    def backward_step(step, carry):
        incoming, normed_buf, grad_buf = carry
        batch = step - (num_sections - 1 - section_pos)
        valid = jnp.logical_and(batch >= 0, batch < num_batches)
        slot = jnp.clip(batch, 0, num_batches - 1)

        def backward_compute(buffers):
            normed_now, grad_now = buffers
            state = pick(stash["states"], slot)
            normed = pick(normed_now, slot)
            preact = pick(stash["preact"], slot)
            result = state + activate(preact)
            upstream = jnp.where(is_last, result * loss_scale, incoming.astype(jnp.float32))
            grad_pre = jax.vjp(activate, preact)[1](upstream)[0].astype(jnp.bfloat16)
            grad_normed = lax.dot_general(
                grad_pre, layer_weight, (((1,), (1,)), ((), ())), preferred_element_type=jnp.float32
            )
            norm_map = partial(normalize, norm_gain=layer_gain)
            grad_state = upstream + jax.vjp(norm_map, state)[1](grad_normed)[0]
            sent = grad_state.astype(jnp.bfloat16)
            return (sent, (place(normed_now, normed, slot), place(grad_now, grad_pre, slot)))

        def backward_skip(buffers):
            return (zero_act, buffers)

        sent, buffers = lax.cond(valid, backward_compute, backward_skip, (normed_buf, grad_buf))
        outgoing = from_behind(sent, "section", -1)
        return (outgoing, buffers[0], buffers[1])

    unused_grad, normed_buf, grad_buf = lax.fori_loop(
        0, steps_total, backward_step, (zero_act, normed_init, grad_init)
    )
    normed_rows = normed_buf.reshape(rows_total, width)
    grad_rows = grad_buf.reshape(rows_total, width)
    replicas = lax.axis_size("dp")
    share = width // replicas
    columns = lax.all_to_all(normed_rows, "dp", split_axis=1, concat_axis=0, tiled=True)
    block_rows = lax.all_gather(grad_rows, "dp", axis=0, tiled=True)
    shard_count = block_rows.shape[0] // rows_total
    cols = columns
    cols = cols.reshape(shard_count, rows_total, share)
    grads_split = block_rows.reshape(shard_count, rows_total, width)
    replica_sums = jnp.einsum(
        "krs,krd->ksd", cols, grads_split, preferred_element_type=jnp.float32
    ).astype(jnp.bfloat16)
    replica_sums = lax.optimization_barrier(replica_sums)
    summed = jnp.sum(replica_sums.astype(jnp.float32), axis=0)
    return (stash["results"][None], summed.astype(jnp.bfloat16)[None])


CORES = 2
MESH = pl.DeviceIdType.MESH
VMEM_LIMIT = 67_043_328


def step_kernel(
    sections,
    replicas,
    chunk,
    tile,
    ids,
    inp,
    sto,
    gain,
    w_hbm,
    out_res,
    out_dw,
    w,
    state,
    slope,
    up,
    gn,
    sf,
    rf,
    sb,
    rb,
    nloc,
    nall,
    gall,
    topart,
    frompart,
    w_sem,
    f_send,
    f_recv,
    b_send,
    b_recv,
    n_send,
    n_recv,
    up_send,
    down_send,
    g_recv,
    p_send,
    p_recv,
):
    rows_total, width = inp.shape
    tokens = sto.shape[2]
    chunks = rows_total // chunk
    tiles = width // tile
    groups = replicas // CORES
    share = width // replicas
    pair = share * CORES
    sub = 16
    sec = lax.axis_index("section")
    dp = lax.axis_index("dp")
    z = dp // CORES
    core = dp % CORES
    partner = z * CORES + (1 - core)
    is_last = sec == sections - 1
    not_last = sec < sections - 1
    loss_scale = 1.0 / math.sqrt(replicas * rows_total)
    f32 = jnp.float32
    bf16 = jnp.bfloat16

    def cols_of(n):
        return pl.ds(pl.multiple_of(n * tile, tile), tile)

    def rows_of(c):
        return pl.ds(pl.multiple_of(c * chunk, chunk), chunk)

    def peer(d):
        return lax.rem(z + d, groups)

    def weight_copy(n):
        return pltpu.make_async_copy(w_hbm.at[:, cols_of(n)], w.at[:, cols_of(n)], w_sem.at[n])

    def f_copy(c, n):
        return pltpu.make_async_remote_copy(
            src_ref=sf.at[rows_of(c), cols_of(n)],
            dst_ref=rf.at[rows_of(c), cols_of(n)],
            send_sem=f_send.at[c, n],
            recv_sem=f_recv.at[c, n],
            device_id={"section": sec + 1},
            device_id_type=MESH,
        )

    def b_copy(c):
        return pltpu.make_async_remote_copy(
            src_ref=sb.at[rows_of(c), :],
            dst_ref=rb.at[rows_of(c), :],
            send_sem=b_send.at[c],
            recv_sem=b_recv.at[c],
            device_id={"section": sec - 1},
            device_id_type=MESH,
        )

    def n_copy(c, src, dst):
        return pltpu.make_async_remote_copy(
            src_ref=nloc.at[rows_of(c), pl.ds(pl.multiple_of(dst * pair, 128), pair)],
            dst_ref=nall.at[src, rows_of(c), :],
            send_sem=n_send.at[c, dst],
            recv_sem=n_recv.at[c, src],
            device_id={"dp": dst * CORES + core},
            device_id_type=MESH,
        )

    def line_copy(c, src, dst, send_sem):
        return pltpu.make_async_remote_copy(
            src_ref=gall.at[src, rows_of(c), :],
            dst_ref=gall.at[src, rows_of(c), :],
            send_sem=send_sem.at[c, src],
            recv_sem=g_recv.at[c, src],
            device_id={"dp": dst * CORES + core},
            device_id_type=MESH,
        )

    def up_copy(c, src):
        return line_copy(c, src, z + 1, up_send)

    def down_copy(c, src):
        return line_copy(c, src, z - 1, down_send)

    has_up = z < groups - 1
    has_down = z > 0

    def p_copy(n):
        return pltpu.make_async_remote_copy(
            src_ref=topart.at[:, cols_of(n)],
            dst_ref=frompart.at[:, cols_of(n)],
            send_sem=p_send.at[n],
            recv_sem=p_recv.at[n],
            device_id={"dp": partner},
            device_id_type=MESH,
        )

    @pl.loop(0, tiles)
    def _(n):
        weight_copy(n).start()

    barrier = pltpu.get_barrier_semaphore()

    @pl.loop(1, groups)
    def _(d):
        pl.semaphore_signal(
            barrier, inc=1, device_id={"dp": peer(d) * CORES + core}, device_id_type=MESH
        )

    pl.semaphore_signal(barrier, inc=1, device_id={"dp": partner}, device_id_type=MESH)

    @pl.when(sec > 0)
    def _():
        pl.semaphore_signal(barrier, inc=1, device_id={"section": sec - 1}, device_id_type=MESH)

    @pl.when(not_last)
    def _():
        pl.semaphore_signal(barrier, inc=1, device_id={"section": sec + 1}, device_id_type=MESH)

    neighbours = jnp.minimum(sec, 1) + jnp.minimum(sections - 1 - sec, 1)
    pl.semaphore_wait(barrier, groups + neighbours)

    def forward(c):
        rows = rows_of(c)
        row0 = c * chunk
        slot = row0 // tokens
        off = row0 - slot * tokens
        sid = ids[0, slot]

        @pl.when(sec == 0)
        def _():
            @pl.loop(0, chunk // sub)
            def _(i):
                at = pl.ds(pl.multiple_of(row0 + i * sub, sub), sub)
                state[at, :] = inp[at, :].astype(f32)

        @pl.when(sec > 0)
        def _():
            @pl.loop(0, tiles)
            def _(n):
                f_copy(c, n).wait_recv()

            @pl.loop(0, chunk // sub)
            def _(i):
                at = pl.ds(pl.multiple_of(row0 + i * sub, sub), sub)
                here = pl.ds(pl.multiple_of(off + i * sub, sub), sub)
                state[at, :] = sto[0, sid, here, :].astype(f32) + rf[at, :].astype(f32)

        @pl.loop(0, chunk // sub)
        def _(i):
            at = pl.ds(pl.multiple_of(row0 + i * sub, sub), sub)
            values = state[at, :]
            centred = values - jnp.mean(values, axis=-1, keepdims=True)
            variance = jnp.mean(centred * centred, axis=-1, keepdims=True)
            nloc[at, :] = (centred * lax.rsqrt(variance + epsilon) * gain[...]).astype(bf16)

        @pl.loop(1, groups)
        def _(d):
            n_copy(c, z, peer(d)).start()

        nall[z, rows, :] = nloc[rows, pl.ds(pl.multiple_of(z * pair, 128), pair)]

        @pl.loop(0, tiles)
        def _(n):
            cols = cols_of(n)

            @pl.when(c == 0)
            def _():
                weight_copy(n).wait()

            pre = jnp.dot(nloc[rows, :], w[:, cols], preferred_element_type=f32)
            cdf = 0.5 * (1.0 + lax.erf(pre * math.sqrt(0.5)))
            result = state[rows, cols] + pre * cdf
            slope[rows, cols] = cdf + pre * (
                jnp.exp(-0.5 * pre * pre) * (1.0 / math.sqrt(2.0 * math.pi))
            )
            out_res[rows, cols] = result.astype(bf16)

            @pl.when(is_last)
            def _():
                up[:, cols] = result * loss_scale

            @pl.when(not_last)
            def _():
                here = pl.ds(pl.multiple_of(off, chunk), chunk)
                delta = result - sto[1, sid, here, cols].astype(f32)
                sf[rows, cols] = jnp.clip(delta, -delta_bound, delta_bound).astype(bf16)
                f_copy(c, n).start()

    def backward(c):
        rows = rows_of(c)

        @pl.when(not_last)
        def _():
            b_copy(c).wait_recv()
            up[...] = rb[rows, :].astype(f32)

        @pl.loop(0, tiles)
        def _(n):
            cols = cols_of(n)
            gall[z, rows, cols] = (slope[rows, cols] * up[:, cols]).astype(bf16)

        @pl.when(has_up)
        def _():
            up_copy(c, z).start()

        @pl.when(has_down)
        def _():
            down_copy(c, z).start()

        @pl.when(sec > 0)
        def _():
            @pl.loop(0, tiles)
            def _(n):
                cols = cols_of(n)
                gn[:, cols] = lax.dot_general(
                    gall[z, rows, :],
                    w[cols, :],
                    (((1,), (1,)), ((), ())),
                    preferred_element_type=f32,
                )

            @pl.loop(0, chunk // sub)
            def _(i):
                at = pl.ds(pl.multiple_of(c * chunk + i * sub, sub), sub)
                here = pl.ds(pl.multiple_of(i * sub, sub), sub)
                values = state[at, :]
                centred = values - jnp.mean(values, axis=-1, keepdims=True)
                variance = jnp.mean(centred * centred, axis=-1, keepdims=True)
                scale = lax.rsqrt(variance + epsilon)
                unit = centred * scale
                grad = gn[here, :] * gain[...]
                first = jnp.mean(grad, axis=-1, keepdims=True)
                second = jnp.mean(grad * unit, axis=-1, keepdims=True)
                sb[at, :] = (up[here, :] + scale * (grad - first - unit * second)).astype(bf16)

            b_copy(c).start()

    lag = jnp.minimum(2 * (sections - 1 - sec), chunks)

    @pl.loop(0, 2 * chunks)
    def _(t):
        @pl.when(t < chunks)
        def _():
            forward(t)

        back = t - lag

        @pl.when(jnp.logical_and(back >= 0, back < chunks))
        def _():
            backward(back)

    @pl.loop(1, groups)
    def _(d):
        below = z - d
        above = z + d

        @pl.loop(0, chunks)
        def _(c):
            @pl.when(below >= 0)
            def _():
                up_copy(c, below).wait_recv()

                @pl.when(has_up)
                def _():
                    up_copy(c, below).start()

            @pl.when(above < groups)
            def _():
                down_copy(c, above).wait_recv()

                @pl.when(has_down)
                def _():
                    down_copy(c, above).start()

    @pl.loop(0, chunks)
    def _(c):
        @pl.loop(1, groups)
        def _(d):
            n_copy(c, peer(d), z).wait_recv()

    def block(half, n):
        left = nall[:, :, pl.ds(pl.multiple_of(half * share, 128), share)]
        left = left.reshape(groups * rows_total, share)
        right = gall[:, :, cols_of(n)].reshape(groups * rows_total, tile)
        return lax.dot_general(
            left, right, (((0,), (0,)), ((), ())), preferred_element_type=f32
        )

    @pl.loop(0, tiles)
    def _(n):
        topart[:, cols_of(n)] = block(1 - core, n).astype(bf16)
        p_copy(n).start()

    @pl.loop(0, tiles)
    def _(n):
        own = block(core, n)
        p_copy(n).wait_recv()
        out_dw[:, cols_of(n)] = (own + frompart[:, cols_of(n)].astype(f32)).astype(bf16)

    @pl.loop(0, tiles)
    def _(n):
        p_copy(n).wait_send()

    @pl.loop(0, chunks)
    def _(c):
        @pl.loop(1, groups)
        def _(d):
            n_copy(c, z, peer(d)).wait_send()

        @pl.loop(0, groups)
        def _(src):
            @pl.when(jnp.logical_and(has_up, src <= z))
            def _():
                up_copy(c, src).wait_send()

            @pl.when(jnp.logical_and(has_down, src >= z))
            def _():
                down_copy(c, src).wait_send()

        @pl.when(not_last)
        def _():
            @pl.loop(0, tiles)
            def _(n):
                f_copy(c, n).wait_send()

        @pl.when(sec > 0)
        def _():
            b_copy(c).wait_send()


def fused_step(inputs, sample_ids, stored, weight, norm_gain):
    sections = lax.axis_size("section")
    replicas = lax.axis_size("dp")
    batches, tokens, width = inputs.shape
    rows = batches * tokens
    chunk, tile = tokens // 2, 512
    chunks, tiles = rows // chunk, width // tile
    groups = replicas // CORES
    share = width // replicas
    pair = share * CORES
    bf16, f32 = jnp.bfloat16, jnp.float32
    vmem = pl.BlockSpec(memory_space=pltpu.VMEM)
    dma = pltpu.SemaphoreType.DMA
    results, grads = pl.pallas_call(
        partial(step_kernel, sections, replicas, chunk, tile),
        out_shape=(
            jax.ShapeDtypeStruct((rows, width), bf16),
            jax.ShapeDtypeStruct((share, width), bf16),
        ),
        in_specs=[
            pl.BlockSpec(memory_space=pltpu.SMEM),
            vmem,
            vmem,
            vmem,
            pl.BlockSpec(memory_space=pl.ANY),
        ],
        out_specs=(vmem, vmem),
        scratch_shapes=[
            pltpu.VMEM((width, width), bf16),
            pltpu.VMEM((rows, width), f32),
            pltpu.VMEM((rows, width), f32),
            pltpu.VMEM((chunk, width), f32),
            pltpu.VMEM((chunk, width), f32),
            pltpu.VMEM((rows, width), bf16),
            pltpu.VMEM((rows, width), bf16),
            pltpu.VMEM((rows, width), bf16),
            pltpu.VMEM((rows, width), bf16),
            pltpu.VMEM((rows, width), bf16),
            pltpu.VMEM((groups, rows, pair), bf16),
            pltpu.VMEM((groups, rows, width), bf16),
            pltpu.VMEM((share, width), bf16),
            pltpu.VMEM((share, width), bf16),
            dma((tiles,)),
            dma((chunks, tiles)),
            dma((chunks, tiles)),
            dma((chunks,)),
            dma((chunks,)),
            dma((chunks, groups)),
            dma((chunks, groups)),
            dma((chunks, groups)),
            dma((chunks, groups)),
            dma((chunks, groups)),
            dma((tiles,)),
            dma((tiles,)),
        ],
        compiler_params=pltpu.CompilerParams(
            collective_id=0, has_side_effects=True, vmem_limit_bytes=VMEM_LIMIT
        ),
    )(sample_ids, inputs.reshape(rows, width), stored[0], norm_gain, weight[0])
    return results.reshape(1, batches, tokens, width), grads[None]


def fits(inputs, replicas):
    batches, tokens, width = inputs.shape
    rows = batches * tokens
    groups = replicas // CORES
    held = 2 * width * width + rows * width * (8 + 2 * (10 + groups)) + 8 * tokens * width
    held += 2 * rows * width + 4 * 2 * width * width // replicas
    aligned = width % 512 == 0 and tokens % 32 == 0 and (width // replicas) % 128 == 0
    return replicas % CORES == 0 and aligned and held < VMEM_LIMIT


def step(inputs, sample_ids, stored, weight, norm_gain):
    run = fused_step if fits(inputs, lax.axis_size("dp")) else per_device
    return run(inputs, sample_ids, stored, weight, norm_gain)


def solution(mesh):
    return jax.shard_map(
        step,
        mesh=mesh,
        in_specs=(
            P("dp", None, None),
            P("dp", None),
            P("section", None, "dp", None, None),
            P("section", None, None),
            P("section", None),
        ),
        out_specs=(P("section", "dp", None, None), P("section", "dp", None)),
        check_vma=False,
    )
```

profile of v0, /device:TPU:0, one launch (start us, length us, event | category | flops | bytes accessed | tf_op | source)
XLA Modules:
  0.0 221.7 jit_solution(10758954953868344515)
XLA Ops:
  0.6 216.9 %shard_map.68 = (bf16[256,3072]{1,0:T(8,128)(2,1)}, bf16[384,3072]{1,0:T(8,128)(2,1)}) custom-call(s32[1,2]{1,0:T(1,128)} %ids.1, bf16[256,3072]{1,0:T(8,128)(2,1)} %bitcast.9, bf16[2,2,128,3072]{3,2,1,0:T(8,128)(2,1)} %bitcast.6, f32[1,3072]{1,0:T(1,128)} %gain.1, bf16[3072,3072]{1,0:T(8,128)(2,1)} %bitcast.5), custom_call_target="tpu_custom_call" | custom-call | tf_op jit(solution)/shard_map/pallas_call | solution.py:534
  217.5 0.0 copy-start
  217.5 2.8 %copy.9 = bf16[1,2,128,3072]{3,2,1,0:T(8,128)(2,1)} copy(bf16[1,2,128,3072]{3,2,1,0:T(8,128)(2,1)} %bitcast.8) | data formatting | bytes 3145728
  220.3 0.0 copy-done
  220.3 1.4 copy.10
Async XLA Ops:
  217.5 2.8 %copy-start = (bf16[384,3072]{1,0:T(8,128)(2,1)S(1)}, bf16[384,3072]{1,0:T(8,128)(2,1)}, u32[]{:S(2)}) copy-start(bf16[384,3072]{1,0:T(8,128)(2,1)} %get-tuple-element.5) | copy-start | bytes 7077892
where the time goes:
time: 222 us
  Pallas kernels  217 us (98%)
  local copies, waits for them, and re-layouts  4.21 us (2%)
    pallas_call x1, Pallas kernels, fused_step(): pl.pallas_call(partial(step_kernel, sections, replicas, chunk, tile), out...  217 us

commit v1 on v0

--- a/solution.py
+++ b/solution.py
@@ -1,3 +1,4 @@
+from contextlib import nullcontext
 from functools import partial
 import math
 
@@ -155,18 +156,26 @@
 VMEM_LIMIT = 67_043_328
 
 
+def scope(name):
+    return nullcontext()
+
+
 def step_kernel(
     sections,
     replicas,
     chunk,
     tile,
+    parts,
     ids,
-    inp,
-    sto,
+    inp_hbm,
+    sto_hbm,
     gain,
     w_hbm,
     out_res,
     out_dw,
+    inp,
+    kept,
+    sent,
     w,
     state,
     slope,
@@ -181,6 +190,7 @@
     gall,
     topart,
     frompart,
+    in_sem,
     w_sem,
     f_send,
     f_recv,
@@ -188,20 +198,23 @@
     b_recv,
     n_send,
     n_recv,
-    up_send,
-    down_send,
+    hub_send,
+    mate_send,
+    relay_send,
     g_recv,
     p_send,
     p_recv,
 ):
     rows_total, width = inp.shape
-    tokens = sto.shape[2]
+    tokens = sent.shape[1]
     chunks = rows_total // chunk
     tiles = width // tile
     groups = replicas // CORES
     share = width // replicas
     pair = share * CORES
+    wide = width // parts
     sub = 16
+    subs = chunk // sub
     sec = lax.axis_index("section")
     dp = lax.axis_index("dp")
     z = dp // CORES
@@ -212,18 +225,41 @@
     loss_scale = 1.0 / math.sqrt(replicas * rows_total)
     f32 = jnp.float32
     bf16 = jnp.bfloat16
+    half = z // 2
+    mate = z + 1 - 2 * lax.rem(z, 2)
+    far_hub = 2 - half
+    far_first = 2 * (1 - half)
+    is_hub = jnp.logical_or(z == 1, z == 2)
 
     def cols_of(n):
         return pl.ds(pl.multiple_of(n * tile, tile), tile)
 
+    def part_of(p):
+        return pl.ds(pl.multiple_of(p * wide, wide), wide)
+
     def rows_of(c):
         return pl.ds(pl.multiple_of(c * chunk, chunk), chunk)
 
+    def sub_of(c, i):
+        return pl.ds(pl.multiple_of(c * chunk + i * sub, sub), sub)
+
     def peer(d):
         return lax.rem(z + d, groups)
 
+    def at_z(d):
+        return {"dp": d * CORES + core}
+
     def weight_copy(n):
         return pltpu.make_async_copy(w_hbm.at[:, cols_of(n)], w.at[:, cols_of(n)], w_sem.at[n])
+
+    def inp_copy():
+        return pltpu.make_async_copy(inp_hbm, inp, in_sem.at[0])
+
+    def kept_copy():
+        return pltpu.make_async_copy(sto_hbm.at[0], kept, in_sem.at[1])
+
+    def sent_copy():
+        return pltpu.make_async_copy(sto_hbm.at[1], sent, in_sem.at[2])
 
     def f_copy(c, n):
         return pltpu.make_async_remote_copy(
@@ -235,12 +271,12 @@
             device_id_type=MESH,
         )
 
-    def b_copy(c):
+    def b_copy(c, i):
         return pltpu.make_async_remote_copy(
-            src_ref=sb.at[rows_of(c), :],
-            dst_ref=rb.at[rows_of(c), :],
-            send_sem=b_send.at[c],
-            recv_sem=b_recv.at[c],
+            src_ref=sb.at[sub_of(c, i), :],
+            dst_ref=rb.at[sub_of(c, i), :],
+            send_sem=b_send.at[c, i],
+            recv_sem=b_recv.at[c, i],
             device_id={"section": sec - 1},
             device_id_type=MESH,
         )
@@ -251,28 +287,28 @@
             dst_ref=nall.at[src, rows_of(c), :],
             send_sem=n_send.at[c, dst],
             recv_sem=n_recv.at[c, src],
-            device_id={"dp": dst * CORES + core},
+            device_id=at_z(dst),
             device_id_type=MESH,
         )
 
-    def line_copy(c, src, dst, send_sem):
+    def g_copy(c, p, src, dst, send_sem):
         return pltpu.make_async_remote_copy(
-            src_ref=gall.at[src, rows_of(c), :],
-            dst_ref=gall.at[src, rows_of(c), :],
-            send_sem=send_sem.at[c, src],
-            recv_sem=g_recv.at[c, src],
-            device_id={"dp": dst * CORES + core},
+            src_ref=gall.at[src, rows_of(c), part_of(p)],
+            dst_ref=gall.at[src, rows_of(c), part_of(p)],
+            send_sem=send_sem,
+            recv_sem=g_recv.at[c, src, p],
+            device_id=at_z(dst),
             device_id_type=MESH,
         )
 
-    def up_copy(c, src):
-        return line_copy(c, src, z + 1, up_send)
-
-    def down_copy(c, src):
-        return line_copy(c, src, z - 1, down_send)
-
-    has_up = z < groups - 1
-    has_down = z > 0
+    def to_hub(c, p):
+        return g_copy(c, p, z, far_hub, hub_send.at[c, p])
+
+    def to_mate(c, p):
+        return g_copy(c, p, z, mate, mate_send.at[c, p])
+
+    def relayed(c, p, j):
+        return g_copy(c, p, far_first + j, mate, relay_send.at[c, p, j])
 
     def p_copy(n):
         return pltpu.make_async_remote_copy(
@@ -284,30 +320,59 @@
             device_id_type=MESH,
         )
 
+    barrier = pltpu.get_barrier_semaphore()
+
+    @pl.loop(1, groups)
+    def _(d):
+        pl.semaphore_signal(barrier, inc=1, device_id=at_z(peer(d)), device_id_type=MESH)
+
+    pl.semaphore_signal(barrier, inc=1, device_id={"dp": partner}, device_id_type=MESH)
+
+    @pl.when(sec > 0)
+    def _():
+        pl.semaphore_signal(barrier, inc=1, device_id={"section": sec - 1}, device_id_type=MESH)
+
+    @pl.when(not_last)
+    def _():
+        pl.semaphore_signal(barrier, inc=1, device_id={"section": sec + 1}, device_id_type=MESH)
+
+    inp_copy().start()
+    sent_copy().start()
+
     @pl.loop(0, tiles)
     def _(n):
         weight_copy(n).start()
 
-    barrier = pltpu.get_barrier_semaphore()
-
-    @pl.loop(1, groups)
-    def _(d):
-        pl.semaphore_signal(
-            barrier, inc=1, device_id={"dp": peer(d) * CORES + core}, device_id_type=MESH
-        )
-
-    pl.semaphore_signal(barrier, inc=1, device_id={"dp": partner}, device_id_type=MESH)
+    kept_copy().start()
+
+    def norm_rows(at):
+        values = state[at, :]
+        centred = values - jnp.mean(values, axis=-1, keepdims=True)
+        variance = jnp.mean(centred * centred, axis=-1, keepdims=True)
+        nloc[at, :] = (centred * lax.rsqrt(variance + epsilon) * gain[...]).astype(bf16)
+
+    def first_norm(c):
+        @pl.loop(0, subs)
+        def _(i):
+            at = sub_of(c, i)
+            state[at, :] = inp[at, :].astype(f32)
+            norm_rows(at)
+
+    inp_copy().wait()
+
+    @pl.when(sec == 0)
+    def _():
+        first_norm(0)
+
+    sent_copy().wait()
 
     @pl.when(sec > 0)
     def _():
-        pl.semaphore_signal(barrier, inc=1, device_id={"section": sec - 1}, device_id_type=MESH)
-
-    @pl.when(not_last)
-    def _():
-        pl.semaphore_signal(barrier, inc=1, device_id={"section": sec + 1}, device_id_type=MESH)
+        kept_copy().wait()
 
     neighbours = jnp.minimum(sec, 1) + jnp.minimum(sections - 1 - sec, 1)
-    pl.semaphore_wait(barrier, groups + neighbours)
+    with scope("bar"):
+        pl.semaphore_wait(barrier, groups + neighbours)
 
     def forward(c):
         rows = rows_of(c)
@@ -316,32 +381,24 @@
         off = row0 - slot * tokens
         sid = ids[0, slot]
 
-        @pl.when(sec == 0)
+        @pl.when(jnp.logical_and(sec == 0, c > 0))
         def _():
-            @pl.loop(0, chunk // sub)
-            def _(i):
-                at = pl.ds(pl.multiple_of(row0 + i * sub, sub), sub)
-                state[at, :] = inp[at, :].astype(f32)
+            first_norm(c)
 
         @pl.when(sec > 0)
         def _():
-            @pl.loop(0, tiles)
-            def _(n):
-                f_copy(c, n).wait_recv()
-
-            @pl.loop(0, chunk // sub)
-            def _(i):
-                at = pl.ds(pl.multiple_of(row0 + i * sub, sub), sub)
-                here = pl.ds(pl.multiple_of(off + i * sub, sub), sub)
-                state[at, :] = sto[0, sid, here, :].astype(f32) + rf[at, :].astype(f32)
-
-        @pl.loop(0, chunk // sub)
-        def _(i):
-            at = pl.ds(pl.multiple_of(row0 + i * sub, sub), sub)
-            values = state[at, :]
-            centred = values - jnp.mean(values, axis=-1, keepdims=True)
-            variance = jnp.mean(centred * centred, axis=-1, keepdims=True)
-            nloc[at, :] = (centred * lax.rsqrt(variance + epsilon) * gain[...]).astype(bf16)
+            with scope("fwait"):
+                @pl.loop(0, tiles)
+                def _(n):
+                    f_copy(c, n).wait_recv()
+
+            with scope("fnorm"):
+                @pl.loop(0, subs)
+                def _(i):
+                    at = sub_of(c, i)
+                    here = pl.ds(pl.multiple_of(off + i * sub, sub), sub)
+                    state[at, :] = kept[sid, here, :].astype(f32) + rf[at, :].astype(f32)
+                    norm_rows(at)
 
         @pl.loop(1, groups)
         def _(d):
@@ -349,118 +406,106 @@
 
         nall[z, rows, :] = nloc[rows, pl.ds(pl.multiple_of(z * pair, 128), pair)]
 
-        @pl.loop(0, tiles)
-        def _(n):
-            cols = cols_of(n)
-
-            @pl.when(c == 0)
-            def _():
-                weight_copy(n).wait()
-
-            pre = jnp.dot(nloc[rows, :], w[:, cols], preferred_element_type=f32)
-            cdf = 0.5 * (1.0 + lax.erf(pre * math.sqrt(0.5)))
-            result = state[rows, cols] + pre * cdf
-            slope[rows, cols] = cdf + pre * (
-                jnp.exp(-0.5 * pre * pre) * (1.0 / math.sqrt(2.0 * math.pi))
-            )
-            out_res[rows, cols] = result.astype(bf16)
-
-            @pl.when(is_last)
-            def _():
+        with scope("fmm"):
+            for n in range(tiles):
+                cols = pl.ds(n * tile, tile)
+
+                @pl.when(c == 0)
+                def _():
+                    weight_copy(n).wait()
+
+                pre = jnp.dot(nloc[rows, :], w[:, cols], preferred_element_type=f32)
+                cdf = 0.5 * (1.0 + lax.erf(pre * math.sqrt(0.5)))
+                result = state[rows, cols] + pre * cdf
+                slope[rows, cols] = cdf + pre * (
+                    jnp.exp(-0.5 * pre * pre) * (1.0 / math.sqrt(2.0 * math.pi))
+                )
+                out_res[rows, cols] = result.astype(bf16)
                 up[:, cols] = result * loss_scale
-
-            @pl.when(not_last)
-            def _():
                 here = pl.ds(pl.multiple_of(off, chunk), chunk)
-                delta = result - sto[1, sid, here, cols].astype(f32)
+                delta = result - sent[sid, here, cols].astype(f32)
                 sf[rows, cols] = jnp.clip(delta, -delta_bound, delta_bound).astype(bf16)
-                f_copy(c, n).start()
+
+                @pl.when(not_last)
+                def _():
+                    f_copy(c, n).start()
 
     def backward(c):
         rows = rows_of(c)
 
         @pl.when(not_last)
         def _():
-            b_copy(c).wait_recv()
+            with scope("bwait"):
+                @pl.loop(0, subs)
+                def _(i):
+                    b_copy(c, i).wait_recv()
             up[...] = rb[rows, :].astype(f32)
 
-        @pl.loop(0, tiles)
-        def _(n):
-            cols = cols_of(n)
+        @pl.loop(0, parts)
+        def _(p):
+            cols = part_of(p)
             gall[z, rows, cols] = (slope[rows, cols] * up[:, cols]).astype(bf16)
-
-        @pl.when(has_up)
-        def _():
-            up_copy(c, z).start()
-
-        @pl.when(has_down)
-        def _():
-            down_copy(c, z).start()
+            to_hub(c, p).start()
+            to_mate(c, p).start()
 
         @pl.when(sec > 0)
         def _():
-            @pl.loop(0, tiles)
-            def _(n):
-                cols = cols_of(n)
-                gn[:, cols] = lax.dot_general(
-                    gall[z, rows, :],
-                    w[cols, :],
-                    (((1,), (1,)), ((), ())),
-                    preferred_element_type=f32,
-                )
-
-            @pl.loop(0, chunk // sub)
-            def _(i):
-                at = pl.ds(pl.multiple_of(c * chunk + i * sub, sub), sub)
-                here = pl.ds(pl.multiple_of(i * sub, sub), sub)
-                values = state[at, :]
-                centred = values - jnp.mean(values, axis=-1, keepdims=True)
-                variance = jnp.mean(centred * centred, axis=-1, keepdims=True)
-                scale = lax.rsqrt(variance + epsilon)
-                unit = centred * scale
-                grad = gn[here, :] * gain[...]
-                first = jnp.mean(grad, axis=-1, keepdims=True)
-                second = jnp.mean(grad * unit, axis=-1, keepdims=True)
-                sb[at, :] = (up[here, :] + scale * (grad - first - unit * second)).astype(bf16)
-
-            b_copy(c).start()
-
-    lag = jnp.minimum(2 * (sections - 1 - sec), chunks)
+            with scope("bmm"):
+                for n in range(tiles):
+                    cols = pl.ds(n * tile, tile)
+                    turned = lax.dot_general(
+                        w[cols, :],
+                        gall[z, rows, :],
+                        (((1,), (1,)), ((), ())),
+                        preferred_element_type=f32,
+                    )
+                    gn[:, cols] = turned.T
+
+            with scope("bnorm"):
+                @pl.loop(0, subs)
+                def _(i):
+                    at = sub_of(c, i)
+                    here = pl.ds(pl.multiple_of(i * sub, sub), sub)
+                    values = state[at, :]
+                    centred = values - jnp.mean(values, axis=-1, keepdims=True)
+                    variance = jnp.mean(centred * centred, axis=-1, keepdims=True)
+                    scale = lax.rsqrt(variance + epsilon)
+                    unit = centred * scale
+                    grad = gn[here, :] * gain[...]
+                    first = jnp.mean(grad, axis=-1, keepdims=True)
+                    second = jnp.mean(grad * unit, axis=-1, keepdims=True)
+                    sb[at, :] = (up[here, :] + scale * (grad - first - unit * second)).astype(bf16)
+                    b_copy(c, i).start()
+
+    def relay(c, p):
+        @pl.loop(0, 2)
+        def _(j):
+            relayed(c, p, j).wait_recv()
+            relayed(c, p, j).start()
+
+    lag = jnp.where(is_last, 0, jnp.where(sec == sections - 2, chunks // 2 - 1, chunks))
+    hold = jnp.where(sec == 0, 1, 3)
 
     @pl.loop(0, 2 * chunks)
     def _(t):
         @pl.when(t < chunks)
         def _():
-            forward(t)
+            with scope("fwd"):
+                forward(t)
 
         back = t - lag
 
         @pl.when(jnp.logical_and(back >= 0, back < chunks))
         def _():
-            backward(back)
-
-    @pl.loop(1, groups)
-    def _(d):
-        below = z - d
-        above = z + d
-
-        @pl.loop(0, chunks)
-        def _(c):
-            @pl.when(below >= 0)
+            with scope("bwd"):
+                backward(back)
+
+            @pl.when(jnp.logical_and(is_hub, back >= hold))
             def _():
-                up_copy(c, below).wait_recv()
-
-                @pl.when(has_up)
-                def _():
-                    up_copy(c, below).start()
-
-            @pl.when(above < groups)
-            def _():
-                down_copy(c, above).wait_recv()
-
-                @pl.when(has_down)
-                def _():
-                    down_copy(c, above).start()
+                with scope("relay"):
+                    @pl.loop(0, parts)
+                    def _(p):
+                        relay(back - hold, p)
 
     @pl.loop(0, chunks)
     def _(c):
@@ -468,54 +513,86 @@
         def _(d):
             n_copy(c, peer(d), z).wait_recv()
 
-    def block(half, n):
-        left = nall[:, :, pl.ds(pl.multiple_of(half * share, 128), share)]
+    def block(side, n):
+        left = nall[:, :, pl.ds(pl.multiple_of(side * share, 128), share)]
         left = left.reshape(groups * rows_total, share)
         right = gall[:, :, cols_of(n)].reshape(groups * rows_total, tile)
         return lax.dot_general(
             left, right, (((0,), (0,)), ((), ())), preferred_element_type=f32
         )
 
-    @pl.loop(0, tiles)
-    def _(n):
-        topart[:, cols_of(n)] = block(1 - core, n).astype(bf16)
-        p_copy(n).start()
-
-    @pl.loop(0, tiles)
-    def _(n):
-        own = block(core, n)
-        p_copy(n).wait_recv()
-        out_dw[:, cols_of(n)] = (own + frompart[:, cols_of(n)].astype(f32)).astype(bf16)
-
-    @pl.loop(0, tiles)
-    def _(n):
-        p_copy(n).wait_send()
-
-    @pl.loop(0, chunks)
-    def _(c):
-        @pl.loop(1, groups)
-        def _(d):
-            n_copy(c, z, peer(d)).wait_send()
-
-        @pl.loop(0, groups)
-        def _(src):
-            @pl.when(jnp.logical_and(has_up, src <= z))
+    per_part = wide // tile
+
+    @pl.loop(0, parts)
+    def _(p):
+        with scope("gwait"):
+            @pl.when(is_hub)
             def _():
-                up_copy(c, src).wait_send()
-
-            @pl.when(jnp.logical_and(has_down, src >= z))
+                @pl.loop(chunks - hold, chunks)
+                def _(c):
+                    relay(c, p)
+
+            @pl.loop(0, chunks)
+            def _(c):
+                g_copy(c, p, mate, z, mate_send.at[c, p]).wait_recv()
+
+                @pl.when(jnp.logical_not(is_hub))
+                def _():
+                    @pl.loop(0, 2)
+                    def _(j):
+                        g_copy(c, p, far_first + j, z, mate_send.at[c, p]).wait_recv()
+
+        with scope("dw"):
+            @pl.loop(0, per_part)
+            def _(k):
+                n = p * per_part + k
+                topart[:, cols_of(n)] = block(1 - core, n).astype(bf16)
+                p_copy(n).start()
+
+            @pl.loop(0, per_part)
+            def _(k):
+                n = p * per_part + k
+                own = block(core, n)
+                p_copy(n).wait_recv()
+                out_dw[:, cols_of(n)] = (own + frompart[:, cols_of(n)].astype(f32)).astype(bf16)
+
+    @pl.when(sec == 0)
+    def _():
+        kept_copy().wait()
+
+    with scope("drain"):
+        @pl.loop(0, tiles)
+        def _(n):
+            p_copy(n).wait_send()
+
+        @pl.loop(0, chunks)
+        def _(c):
+            @pl.loop(1, groups)
+            def _(d):
+                n_copy(c, z, peer(d)).wait_send()
+
+            @pl.loop(0, parts)
+            def _(p):
+                to_hub(c, p).wait_send()
+                to_mate(c, p).wait_send()
+
+                @pl.when(is_hub)
+                def _():
+                    @pl.loop(0, 2)
+                    def _(j):
+                        relayed(c, p, j).wait_send()
+
+            @pl.when(not_last)
             def _():
-                down_copy(c, src).wait_send()
-
-        @pl.when(not_last)
-        def _():
-            @pl.loop(0, tiles)
-            def _(n):
-                f_copy(c, n).wait_send()
-
-        @pl.when(sec > 0)
-        def _():
-            b_copy(c).wait_send()
+                @pl.loop(0, tiles)
+                def _(n):
+                    f_copy(c, n).wait_send()
+
+            @pl.when(sec > 0)
+            def _():
+                @pl.loop(0, subs)
+                def _(i):
+                    b_copy(c, i).wait_send()
 
 
 def fused_step(inputs, sample_ids, stored, weight, norm_gain):
@@ -523,29 +600,28 @@
     replicas = lax.axis_size("dp")
     batches, tokens, width = inputs.shape
     rows = batches * tokens
-    chunk, tile = tokens // 2, 512
+    chunk, tile, parts = tokens // 4, 512, 3
     chunks, tiles = rows // chunk, width // tile
     groups = replicas // CORES
     share = width // replicas
     pair = share * CORES
     bf16, f32 = jnp.bfloat16, jnp.float32
     vmem = pl.BlockSpec(memory_space=pltpu.VMEM)
+    hbm = pl.BlockSpec(memory_space=pl.ANY)
     dma = pltpu.SemaphoreType.DMA
+    subs = chunk // 16
     results, grads = pl.pallas_call(
-        partial(step_kernel, sections, replicas, chunk, tile),
+        partial(step_kernel, sections, replicas, chunk, tile, parts),
         out_shape=(
             jax.ShapeDtypeStruct((rows, width), bf16),
             jax.ShapeDtypeStruct((share, width), bf16),
         ),
-        in_specs=[
-            pl.BlockSpec(memory_space=pltpu.SMEM),
-            vmem,
-            vmem,
-            vmem,
-            pl.BlockSpec(memory_space=pl.ANY),
-        ],
+        in_specs=[pl.BlockSpec(memory_space=pltpu.SMEM), hbm, hbm, vmem, hbm],
         out_specs=(vmem, vmem),
         scratch_shapes=[
+            pltpu.VMEM((rows, width), bf16),
+            pltpu.VMEM((batches, tokens, width), bf16),
+            pltpu.VMEM((batches, tokens, width), bf16),
             pltpu.VMEM((width, width), bf16),
             pltpu.VMEM((rows, width), f32),
             pltpu.VMEM((rows, width), f32),
@@ -560,16 +636,18 @@
             pltpu.VMEM((groups, rows, width), bf16),
             pltpu.VMEM((share, width), bf16),
             pltpu.VMEM((share, width), bf16),
+            dma((3,)),
             dma((tiles,)),
             dma((chunks, tiles)),
             dma((chunks, tiles)),
-            dma((chunks,)),
-            dma((chunks,)),
+            dma((chunks, subs)),
+            dma((chunks, subs)),
             dma((chunks, groups)),
             dma((chunks, groups)),
-            dma((chunks, groups)),
-            dma((chunks, groups)),
-            dma((chunks, groups)),
+            dma((chunks, parts)),
+            dma((chunks, parts)),
+            dma((chunks, parts, 2)),
+            dma((chunks, groups, parts)),
             dma((tiles,)),
             dma((tiles,)),
         ],
@@ -586,7 +664,7 @@
     groups = replicas // CORES
     held = 2 * width * width + rows * width * (8 + 2 * (10 + groups)) + 8 * tokens * width
     held += 2 * rows * width + 4 * 2 * width * width // replicas
-    aligned = width % 512 == 0 and tokens % 32 == 0 and (width // replicas) % 128 == 0
+    aligned = width % 1536 == 0 and tokens % 32 == 0 and replicas == 4 * CORES and (width // replicas) % 128 == 0
     return replicas % CORES == 0 and aligned and held < VMEM_LIMIT
 
 

time: 222 us -> 191 us (0.86)
  Pallas kernels: 217 us -> 185 us
    pallas_call x1, Pallas kernels: 217 us -> 185 us  [fused_step(): pl.pallas_call(partial(step_kernel, sections, replicas, chunk, tile, part...]
where the time goes in v1:
time: 191 us; the launch traced here: 190 us
  Pallas kernels  185 us (97%)
  local copies, waits for them, and re-layouts  4.21 us (2%)
    pallas_call x1, Pallas kernels, fused_step(): pl.pallas_call(partial(step_kernel, sections, replicas, chunk, tile, part...  185 us
    unnamed x4, local copies, waits for them, and re-layouts  4.21 us

profile of v1, /device:TPU:0, one launch (start us, length us, event | category | flops | bytes accessed | tf_op | source)
XLA Modules:
  0.0 190.3 jit_solution(784662807722443914)
XLA Ops:
  0.6 185.4 %shard_map.68 = (bf16[256,3072]{1,0:T(8,128)(2,1)}, bf16[384,3072]{1,0:T(8,128)(2,1)}) custom-call(s32[1,2]{1,0:T(1,128)} %ids.1, bf16[256,3072]{1,0:T(8,128)(2,1)} %bitcast.9, bf16[2,2,128,3072]{3,2,1,0:T(8,128)(2,1)} %bitcast.6, f32[1,3072]{1,0:T(1,128)} %gain.1, bf16[3072,3072]{1,0:T(8,128)(2,1)} %bitcast.5), custom_call_target="tpu_custom_call" | custom-call | tf_op jit(solution)/shard_map/pallas_call | solution.py:613
  186.1 0.0 copy-start
  186.1 2.8 %copy.9 = bf16[1,2,128,3072]{3,2,1,0:T(8,128)(2,1)} copy(bf16[1,2,128,3072]{3,2,1,0:T(8,128)(2,1)} %bitcast.8) | data formatting | bytes 3145728
  188.9 0.0 copy-done
  188.9 1.4 copy.10
Async XLA Ops:
  186.1 2.8 %copy-start = (bf16[384,3072]{1,0:T(8,128)(2,1)S(1)}, bf16[384,3072]{1,0:T(8,128)(2,1)}, u32[]{:S(2)}) copy-start(bf16[384,3072]{1,0:T(8,128)(2,1)} %get-tuple-element.5) | copy-start | bytes 7077892
